TPU v7x, 32 devices: a whole 2x2x4 slice. The times are simulated.
32 devices in a mesh: row: 8 (over z, x), col: 4 (over y, core).
Axes of the slice: x: 2, y: 2, z: 4, core: 2. Of those that a mesh axis runs over, the one named last changes fastest.
Arguments:
- prior_scores: float32 [12288, 12288], P('row', 'col'), may hold values from 0.001 to 10
- tiles_first: bfloat16 [96, 5, 128, 128], P('row'), may hold values from 0 to 1, as said below
- columns_first: int32 [96, 5], P('row'), may hold values from 0 to 95, as said below
- tiles_second: bfloat16 [96, 5, 128, 128], P('col'), may hold values from 0 to 1, as said below
- columns_second: int32 [96, 5], P('col'), may hold values from 0 to 95, as said below
Outputs:
- alignment: float32 [12288, 12288], P('row', 'col')
Inputs may be any that keep to these rules, and one draw needn't show every extreme that they name: `tiles_first`: in every block row, the block in the first slot has entries of 0.5 or more on its diagonal. `tiles_second`: in every block row, the block in the first slot has entries of 0.5 or more on its diagonal. `columns_first`: each block row lists 5 different block columns. `columns_second`: each block row lists 5 different block columns.
All inputs are finite; a program needn't handle non-finite values.
Results may differ from a plain program's by a relative error of at most 0.0004.
The roundings to bfloat16 on the way count: a program that leaves them out, or rounds other values in their place, can miss the bound.
Values may be sent and summed in bfloat16 or wider, within the bound.
A program may use at most 192 MiB of HBM per device.

v0:
```python
import jax
import jax.numpy as jnp
from jax import lax
from jax.sharding import PartitionSpec as P

ITERS = 2


mixing = 0.8


def second_product(features, tile_set, columns, inverse):
    tile_size = tile_set.shape[2]
    blocks = features.reshape(-1, tile_size, features.shape[1])
    picked = jnp.take(blocks, columns, axis=0)
    result = jnp.einsum("jsoi,jsin->jon", tile_set, picked, preferred_element_type=jnp.float32)
    result = result.reshape(-1, features.shape[1]) * inverse[:, None]
    return result.astype(jnp.bfloat16)


def first_product(slab_data, tile_set, columns, inverse):
    tile_size = tile_set.shape[2]
    blocks = slab_data.reshape(slab_data.shape[0], -1, tile_size)
    picked = jnp.take(blocks, columns, axis=1)
    result = jnp.einsum("cisk,isok->cio", picked, tile_set, preferred_element_type=jnp.float32)
    result = result.reshape(slab_data.shape[0], -1) * inverse[None, :]
    return result.astype(jnp.bfloat16)


def local(prior_scores, tiles_first, columns_first, tiles_second, columns_second):
    prior_cols = prior_scores.T
    row_count = lax.axis_size("row")
    cell_count = float(
        prior_scores.shape[0] * row_count * prior_scores.shape[1] * lax.axis_size("col")
    )
    all_first, all_columns = (
        lax.all_gather(tiles_first, "row", axis=0, tiled=True),
        lax.all_gather(columns_first, "row", axis=0, tiled=True),
    )
    inverse_first = 1.0 / jnp.sum(all_first, axis=(1, 3), dtype=jnp.float32).reshape(-1)
    inverse_second = 1.0 / jnp.sum(tiles_second, axis=(1, 3), dtype=jnp.float32).reshape(-1)
    prior_sum = lax.psum(jnp.sum(prior_cols), ("row", "col"))
    current_state = prior_cols
    for iteration in range(ITERS):
        current = current_state.astype(jnp.bfloat16)
        gathered = lax.all_gather(current, "col", axis=0, tiled=True)
        mixed_cols = second_product(gathered, tiles_second, columns_second, inverse_second)
        slab_data = lax.all_to_all(mixed_cols, "row", split_axis=0, concat_axis=1, tiled=True)
        propagated = first_product(slab_data, all_first, all_columns, inverse_first)
        partial_value = jnp.sum(propagated.astype(jnp.float32))
        returned = lax.all_to_all(propagated, "row", split_axis=1, concat_axis=0, tiled=True)
        slab_sum = lax.psum(partial_value, ("row", "col"))
        grand_total = mixing * slab_sum + (1.0 - mixing) * prior_sum
        updated = mixing * returned.astype(jnp.float32) + (1.0 - mixing) * prior_cols
        current_state = updated / (grand_total / cell_count)
    return current_state.T


def solution(mesh):
    return jax.shard_map(
        local,
        mesh=mesh,
        in_specs=(
            P("row", "col"),
            P("row", None, None, None),
            P("row", None),
            P("col", None, None, None),
            P("col", None),
        ),
        out_specs=P("row", "col"),
        check_vma=False,
    )
```

profile of v0, /device:TPU:10, one launch (start us, length us, event | category | flops | bytes accessed | tf_op | source)
XLA Modules:
  0.0 1960.2 jit_solution(3482156097374935337)
XLA Ops:
  6.5 0.0 all-gather.5.cloned.1.call-start
  6.5 20.0 %fusion.28 = (f32[]{:T(128)}, bf16[3072,1536]{0,1:T(8,128)(2,1)}) fusion(f32[1536,3072]{1,0:T(8,128)} %param.9), kind=kLoop, calls=%fused_computation.55 | loop fusion | flops 9437183 | bytes 28311556 | tf_op jit(solution)/shard_map/reduce_sum | solution.py:42
  26.5 0.0 all-gather.5.cloned.1.call-update
  26.6 0.0 all-gather.7.cloned.1.call-start
  26.6 0.7 all-gather.7.cloned.1.call-update
  27.3 0.0 copy-done.10
  27.3 0.1 copy.33
  27.5 0.1 copy.37
  27.5 0.1 reshape.154
  27.6 2.7 convert_reduce_fusion.3
  30.4 0.0 copy-start.8
  30.4 0.0 copy-start.4
  30.4 224.6 %all-gather.5.cloned.1.call-done = bf16[12288,1536]{0,1:T(8,128)(2,1)} async-done(((bf16[3072,1536]{0,1:T(8,128)(2,1)}), bf16[12288,1536]{0,1:T(8,128)(2,1)}) %all-gather.5.cloned.1.call-update) | async-done | bytes 37748752 | tf_op jit(solution)/shard_map/all_gather | solution.py:46
  255.0 48.9 %copy.36 = bf16[12288,1536]{1,0:T(8,128)(2,1)} copy(bf16[12288,1536]{0,1:T(8,128)(2,1)} %all-gather.5.cloned.1.call-done) | data formatting | bytes 75497472 | tf_op jit(solution)/shard_map/all_gather | solution.py:46
  304.0 0.0 copy-done.4
  304.0 34.9 %gather_fusion = bf16[120,128,1536]{2,1,0:T(8,128)(2,1)} fusion(bf16[96,128,1536]{2,1,0:T(8,128)(2,1)} %bitcast.87, s32[1024]{0:T(1024)S(1)} %pad_clamp_fusion.1), kind=kCustom, calls=%fused_computation.clone | custom fusion | bytes 94372320 | tf_op jit(solution)/shard_map/jit(_take)/gather | solution.py:15
  338.9 0.0 copy-done.14
  338.9 26.3 %fusion.8 = f32[24,1536,128,1]{1,2,3,0:T(8,128)} fusion(bf16[24,5,128,128]{3,2,1,0:T(8,128)(2,1)} %param.12, bf16[24,5,128,1536]{3,2,1,0:T(8,128)(2,1)} %bitcast.93, pred[24,5]{1,0:T(8,128)(4,1)S(1)} %copy.33), kind=kOutput, calls=%fused_computation.12 | convolution fusion | flops 6063390720 | bytes 69992568 | tf_op jit(solution)/shard_map/jsoi,jsin->jon/dot_general | solution.py:16
  365.2 18.6 copy.38
  383.8 0.0 copy-done.8
  383.8 11.6 multiply_convert_fusion.3
  395.4 6.1 all-to-all-start
  401.5 0.0 copy-done.13
  401.5 287.1 %all-gather = s32[8,12,5]{1,2,0:T(8,128)S(1)} all-gather(s32[1,12,5]{1,2,0:T(8,128)S(1)} %bitcast.99), channel_id=1, replica_groups=mesh['row'=8,'col'=4] {'row'}, dimensions={0}, use_global_device_ids=true | all-gather | bytes 2160 | tf_op jit(solution)/shard_map/all_gather | solution.py:38
  688.6 0.1 reshape.153
  688.7 0.1 copy.32
  688.8 0.1 copy.39
  688.9 0.2 reshape.158
  689.1 0.0 copy-start
  689.1 0.0 all-gather.7.cloned.1.call-done
  689.1 6.6 convert_reduce_fusion
  695.8 0.0 copy-start.2
  695.8 0.0 all-to-all-done
  695.8 12.6 copy.40
  708.4 23.7 %gather_fusion.1 = bf16[480,384,128]{2,1,0:T(8,128)(2,1)} fusion(bf16[384,96,128]{2,0,1:T(8,128)(2,1)} %copy.40, s32[1024]{0:T(1024)S(1)} %pad_clamp_fusion), kind=kCustom, calls=%fused_computation.1.clone | custom fusion | bytes 94373760 | tf_op jit(solution)/shard_map/jit(_take)/gather | solution.py:24
  732.1 0.0 copy-done.11
  732.1 31.3 %convert_reduce_fusion.2 = (f32[]{:T(128)}, f32[96,384,128,1]{1,2,3,0:T(8,128)}) fusion(f32[96,128]{1,0:T(8,128)S(1)} %broadcast_divide_fusion, bf16[96,5,128,128]{3,2,1,0:T(8,128)(2,1)} %all-gather.7.cloned.1.call-done, bf16[96,5,384,128]{3,2,1,0:T(8,128)(2,1)} %bitcast.89, pred[96,5]{1,0:T(8,128)(4,1)S(1)} %copy.32), kind=kOutput, calls=%fused_computation.37 | convolution fusion | flops 6082265088 | bytes 81838560 | tf_op jit(solution)/shard_map/cisk,isok->cio/dot_general | solution.py:25
  763.4 0.0 copy-done.2
  763.4 11.8 multiply_convert_fusion.2
  775.2 8.2 all-to-all-start.1
  783.4 0.0 all-gather.9.cloned.1.call-start
  783.4 219.6 %all-reduce = (f32[]{:T(128)}, f32[]{:T(128)}) all-reduce(f32[]{:T(128)} %get-tuple-element.11, f32[]{:T(128)} %get-tuple-element.9), channel_id=1, replica_groups=mesh['row'=8,'col'=4] {'row','col'}, use_global_device_ids=true, to_apply=%region_3.6 | all-reduce | flops 2 | bytes 16 | tf_op jit(solution)/shard_map/psum | solution.py:52
  1004.2 0.0 all-to-all-done.1
  1004.2 12.4 multiply_bitcast_fusion.1
  1016.6 7.6 copy.52
  1024.2 12.7 fusion.21
  1036.9 0.0 all-gather.9.cloned.1.call-update
  1036.9 228.0 %all-gather.9.cloned.1.call-done = bf16[12288,1536]{0,1:T(8,128)(2,1)} async-done(((bf16[3072,1536]{0,1:T(8,128)(2,1)}), bf16[12288,1536]{0,1:T(8,128)(2,1)}) %all-gather.9.cloned.1.call-update) | async-done | bytes 37748752 | tf_op jit(solution)/shard_map/all_gather | solution.py:46
  1265.0 48.7 %copy.42 = bf16[12288,1536]{1,0:T(8,128)(2,1)} copy(bf16[12288,1536]{0,1:T(8,128)(2,1)} %all-gather.9.cloned.1.call-done) | data formatting | bytes 75497472 | tf_op jit(solution)/shard_map/all_gather | solution.py:46
  1313.6 34.9 %gather_fusion.2 = bf16[120,128,1536]{2,1,0:T(8,128)(2,1)} fusion(bf16[96,128,1536]{2,1,0:T(8,128)(2,1)} %bitcast.86, s32[1024]{0:T(1024)S(1)} %copy-done.5), kind=kCustom, calls=%fused_computation.2.clone | custom fusion | bytes 94372320 | tf_op jit(solution)/shard_map/jit(_take)/gather | solution.py:15
  1348.5 24.3 %fusion.5 = f32[24,1536,128,1]{1,2,3,0:T(8,128)} fusion(bf16[24,5,128,128]{3,2,1,0:T(8,128)(2,1)} %param.12, bf16[24,5,128,1536]{3,2,1,0:T(8,128)(2,1)} %bitcast.92, pred[24,5]{1,0:T(8,128)(4,1)S(1)} %copy-done.15), kind=kOutput, calls=%fused_computation.9 | convolution fusion | flops 6063390720 | bytes 69992568 | tf_op jit(solution)/shard_map/jsoi,jsin->jon/dot_general | solution.py:16
  1372.9 18.7 copy.44
  1391.5 7.6 multiply_convert_fusion.1
  1399.1 207.2 %all_to_all.46 = bf16[8,384,1536]{1,2,0:T(8,128)(2,1)} all-to-all(bf16[8,384,1536]{1,2,0:T(8,128)(2,1)S(1)} %multiply_convert_fusion.1), channel_id=1, replica_groups=mesh['row'=8,'col'=4] {'row'}, dimensions={0} | all-to-all | bytes 18874368 | tf_op jit(solution)/shard_map/all_to_all | solution.py:48
  1606.3 12.6 copy.46
  1618.9 23.7 %gather_fusion.3 = bf16[480,384,128]{2,1,0:T(8,128)(2,1)} fusion(bf16[384,96,128]{2,0,1:T(8,128)(2,1)} %copy.46, s32[1024]{0:T(1024)S(1)} %copy-done.1), kind=kCustom, calls=%fused_computation.3.clone | custom fusion | bytes 94373760 | tf_op jit(solution)/shard_map/jit(_take)/gather | solution.py:24
  1642.6 31.3 %convert_reduce_fusion.1 = (f32[]{:T(128)}, f32[96,384,128,1]{1,2,3,0:T(8,128)}) fusion(f32[96,128]{1,0:T(8,128)S(1)} %copy-done.7, bf16[96,5,128,128]{3,2,1,0:T(8,128)(2,1)} %all-gather.7.cloned.1.call-done, bf16[96,5,384,128]{3,2,1,0:T(8,128)(2,1)} %bitcast.88, pred[96,5]{1,0:T(8,128)(4,1)S(1)} %copy-done.12), kind=kOutput, calls=%fused_computation.33 | convolution fusion | flops 6082265088 | bytes 81838560 | tf_op jit(solution)/shard_map/cisk,isok->cio/dot_general | solution.py:25
  1673.9 11.8 multiply_convert_fusion
  1685.7 7.1 all-to-all-start.3
  1692.8 224.7 %psum.23 = f32[]{:T(128)} all-reduce(f32[]{:T(128)} %get-tuple-element.13), channel_id=1, replica_groups=mesh['row'=8,'col'=4] {'row','col'}, use_global_device_ids=true, to_apply=%region_7.10 | all-reduce | flops 1 | bytes 8 | tf_op jit(solution)/shard_map/psum | solution.py:52
  1918.2 0.0 all-to-all-done.3
  1918.2 12.4 multiply_bitcast_fusion
  1930.6 7.6 copy.53
  1938.2 15.5 fusion.23
  (32 shorter events, 0.1 us)
Async XLA Ops:
  6.5 20.8 %copy-start.10 = (s32[24,5]{0,1:T(8,128)S(1)}, s32[24,5]{0,1:T(8,128)}, u32[]{:S(2)}) copy-start(s32[24,5]{0,1:T(8,128)} %param.13) | copy-start | bytes 1444
  6.5 248.5 %all-gather.5.cloned.1.call-start = ((), (), s32[]{:S(2)}) async-start(), calls=%async_computation.4 | async-start | bytes 47185920 | tf_op jit(solution)/shard_map/all_gather | solution.py:46
  26.6 662.6 %all-gather.7.cloned.1.call-start = ((), (), s32[]{:S(2)}) async-start(), calls=%async_computation.5 | async-start | bytes 17694720 | tf_op jit(solution)/shard_map/all_gather | solution.py:37
  27.4 311.4 %copy-start.14 = (pred[24,5]{1,0:T(8,128)(4,1)}, pred[24,5]{1,0:T(8,128)(4,1)S(1)}, u32[]{:S(2)}) copy-start(pred[24,5]{1,0:T(8,128)(4,1)S(1)} %copy.33) | copy-start | bytes 364
  30.4 353.4 %copy-start.8 = (f32[8,384]{1,0:T(8,128)}, f32[8,384]{1,0:T(8,128)S(1)}, u32[]{:S(2)}) copy-start(f32[8,384]{1,0:T(8,128)S(1)} %div.47) | copy-start | bytes 36868
  30.4 273.6 %copy-start.4 = (s32[1024]{0:T(1024)}, s32[1024]{0:T(1024)S(1)}, u32[]{:S(2)}) copy-start(s32[1024]{0:T(1024)S(1)} %pad_clamp_fusion.1) | copy-start | bytes 12292
  383.8 17.6 copy-start.13
  395.4 300.4 %all-to-all-start = ((bf16[8,384,1536]{1,2,0:T(8,128)(2,1)}), bf16[8,384,1536]{1,2,0:T(8,128)(2,1)}, u32[]{:S(2)}, u32[]{:S(2)}) async-start(bf16[8,384,1536]{1,2,0:T(8,128)(2,1)} %multiply_convert_fusion.3), calls=%async_computation | async-start | bytes 18874368 | tf_op jit(solution)/shard_map/all_to_all | solution.py:48
  688.8 43.3 %copy-start.11 = (pred[96,5]{1,0:T(8,128)(4,1)}, pred[96,5]{1,0:T(8,128)(4,1)S(1)}, u32[]{:S(2)}) copy-start(pred[96,5]{1,0:T(8,128)(4,1)S(1)} %copy.32) | copy-start | bytes 1444
  689.1 43.0 %copy-start = (s32[1024]{0:T(1024)}, s32[1024]{0:T(1024)S(1)}, u32[]{:S(2)}) copy-start(s32[1024]{0:T(1024)S(1)} %pad_clamp_fusion) | copy-start | bytes 12292
  695.8 36.3 %copy-start.6 = (f32[96,128]{1,0:T(8,128)}, f32[96,128]{1,0:T(8,128)S(1)}, u32[]{:S(2)}) copy-start(f32[96,128]{1,0:T(8,128)S(1)} %broadcast_divide_fusion) | copy-start | bytes 147460
  695.8 67.6 %copy-start.2 = (f32[8,1536]{1,0:T(8,128)}, f32[8,1536]{1,0:T(8,128)S(1)}, u32[]{:S(2)}) copy-start(f32[8,1536]{1,0:T(8,128)S(1)} %div.50) | copy-start | bytes 147460
  775.2 229.0 %all-to-all-start.1 = ((bf16[384,8,1536]{0,2,1:T(8,128)(2,1)}), bf16[384,8,1536]{0,2,1:T(8,128)(2,1)}, u32[]{:S(2)}, u32[]{:S(2)}) async-start(bf16[384,8,1536]{0,2,1:T(8,128)(2,1)} %multiply_convert_fusion.2), calls=%async_computation.1 | async-start | bytes 18874368 | tf_op jit(solution)/shard_map/all_to_all | solution.py:51
  783.4 481.6 %all-gather.9.cloned.1.call-start = ((), (), s32[]{:S(2)}) async-start(), calls=%async_computation.6 | async-start | bytes 47185920 | tf_op jit(solution)/shard_map/all_gather | solution.py:46
  1036.9 276.7 %copy-start.5 = (s32[1024]{0:T(1024)S(1)}, s32[1024]{0:T(1024)}, u32[]{:S(2)}) copy-start(s32[1024]{0:T(1024)} %copy-done.4) | copy-start | bytes 12292
  1313.6 34.9 %copy-start.15 = (pred[24,5]{1,0:T(8,128)(4,1)S(1)}, pred[24,5]{1,0:T(8,128)(4,1)}, u32[]{:S(2)}) copy-start(pred[24,5]{1,0:T(8,128)(4,1)} %copy-done.14) | copy-start | bytes 364
  1372.9 18.7 copy-start.9
  1399.1 219.8 %copy-start.1 = (s32[1024]{0:T(1024)S(1)}, s32[1024]{0:T(1024)}, u32[]{:S(2)}) copy-start(s32[1024]{0:T(1024)} %copy-done) | copy-start | bytes 12292
  1618.9 23.7 %copy-start.7 = (f32[96,128]{1,0:T(8,128)S(1)}, f32[96,128]{1,0:T(8,128)}, u32[]{:S(2)}) copy-start(f32[96,128]{1,0:T(8,128)} %copy-done.6) | copy-start | bytes 147460
  1618.9 23.7 %copy-start.12 = (pred[96,5]{1,0:T(8,128)(4,1)S(1)}, pred[96,5]{1,0:T(8,128)(4,1)}, u32[]{:S(2)}) copy-start(pred[96,5]{1,0:T(8,128)(4,1)} %copy-done.11) | copy-start | bytes 1444
  1642.6 31.3 %copy-start.3 = (f32[8,1536]{1,0:T(8,128)S(1)}, f32[8,1536]{1,0:T(8,128)}, u32[]{:S(2)}) copy-start(f32[8,1536]{1,0:T(8,128)} %copy-done.2) | copy-start | bytes 147460
  1685.7 232.5 %all-to-all-start.3 = ((bf16[384,8,1536]{0,2,1:T(8,128)(2,1)}), bf16[384,8,1536]{0,2,1:T(8,128)(2,1)}, u32[]{:S(2)}, u32[]{:S(2)}) async-start(bf16[384,8,1536]{0,2,1:T(8,128)(2,1)} %multiply_convert_fusion), calls=%async_computation.3 | async-start | bytes 18874368 | tf_op jit(solution)/shard_map/all_to_all | solution.py:51
Sparse Core Ops, SparseCore 0:
  26.7 228.3 all-gather.4
  257.2 330.5 all-gather.6
  1037.0 227.8 all-gather.8
where the time goes:
time: 1970 us; the launch traced here: 1960 us
  blocking collectives  939 us (48%)
  waiting for transfers between devices  453 us (23%)
  local copies, waits for them, and re-layouts  293 us (15%)
  other arithmetic  125 us (6%)
  matrix products  113 us (6%)
  starting transfers between devices  21.4 us (1%)
    all_gather x2, waiting for transfers between devices, local(): gathered = lax.all_gather(current, 'col', axis=0, tiled=True)  453 us
    psum x2, blocking collectives, local(): slab_sum = lax.psum(partial_value, ('row', 'col'))  444 us
    all_gather x1, blocking collectives, local(): lax.all_gather(columns_first, 'row', axis=0, tiled=True)  287 us
    all_to_all x1, blocking collectives, local(): lax.all_to_all(mixed_cols, 'row', split_axis=0, concat_axis=1, tiled=True)  207 us
    all_gather x2, local copies, waits for them, and re-layouts, local(): gathered = lax.all_gather(current, 'col', axis=0, tiled=True)  97.6 us
    gather x2, local copies, waits for them, and re-layouts, second_product(): picked = jnp.take(blocks, columns, axis=0)  69.8 us
    dot_general x2, matrix products, first_product(): jnp.einsum('cisk,isok->cio', picked, tile_set, preferred_element_type=jnp...  62.6 us
    dot_general x2, matrix products, second_product(): jnp.einsum('jsoi,jsin->jon', tile_set, picked, preferred_element_type=jnp...  50.6 us
  transfers between devices with their start and end apart: 6, of which 2 were waited for; matrix products, arithmetic and copies ran while one was open for 8% of the time, Pallas kernels for 0%

commit v1 on v0

v1 whole, which is shorter than its diff:
```python
import functools

import jax
import jax.numpy as jnp
from jax import lax
from jax.experimental import pallas as pl
from jax.experimental.pallas import tpu as pltpu
from jax.sharding import PartitionSpec as P

ITERS = 2
mixing = 0.8
CHUNKS = 4
SUBS = 4
MESH = pl.DeviceIdType.MESH
VMEM_LIMIT = 60 * 1024 * 1024


def divisor(total, wanted, unit):
    for count in range(wanted, 0, -1):
        if total % (count * unit) == 0:
            return count
    return 1


def comm_kernel(tasks, row_count, col_count, *refs):
    count = len(tasks)
    sources, targets = refs[:count], refs[count : 2 * count]
    scratch = refs[2 * count :]
    me_row, me_col = lax.axis_index("row"), lax.axis_index("col")
    has_gather = any(task[0] == "gather" for task in tasks)
    has_swap = any(task[0] == "swap" for task in tasks)
    paired = col_count % 2 == 0
    stride = 2 if paired else 1
    partner = me_col + 1 - 2 * lax.rem(me_col, 2)

    barrier = pltpu.get_barrier_semaphore()
    greeted = 0
    if has_gather:
        for step in range(1, col_count):
            peer = lax.rem(me_col + step, col_count)
            pl.semaphore_signal(barrier, inc=1, device_id=(me_row, peer), device_id_type=MESH)
            greeted += 1
    if has_swap:
        for step in range(1, row_count):
            peer = lax.rem(me_row + step, row_count)
            pl.semaphore_signal(barrier, inc=1, device_id=(peer, me_col), device_id_type=MESH)
            greeted += 1
    pl.semaphore_wait(barrier, greeted)

    pending = []
    local = []
    forwards = []
    for index, task in enumerate(tasks):
        source, target = sources[index], targets[index]
        bounce, local_sem, send_sem, recv_sem, pair_send, pair_recv = scratch[6 * index : 6 * index + 6]
        if task[0] == "gather":
            rows = source.shape[0]
            subs = divisor(rows, SUBS, 16)
            size = rows // subs
            for sub in range(subs):
                span = pl.ds(sub * size, size)
                for hop in range(1, col_count // stride):
                    peer = lax.rem(me_col + stride * hop, col_count)
                    origin = lax.rem(me_col + col_count - stride * hop, col_count)
                    slot = (hop - 1) * subs + sub
                    copy = pltpu.make_async_remote_copy(
                        src_ref=source.at[span],
                        dst_ref=target.at[me_col, span],
                        send_sem=send_sem.at[slot],
                        recv_sem=recv_sem.at[slot],
                        device_id=(me_row, peer),
                        device_id_type=MESH,
                    )
                    copy.start()
                    forwards.append((copy, target, origin, span, slot, pair_send, pair_recv))
            if paired:
                copy = pltpu.make_async_remote_copy(
                    src_ref=source,
                    dst_ref=target.at[me_col],
                    send_sem=pair_send.at[0],
                    recv_sem=pair_recv.at[0],
                    device_id=(me_row, partner),
                    device_id_type=MESH,
                )
                copy.start()
                pending.append(copy)
            local.append((source, target.at[me_col], bounce, local_sem))
        else:
            start, size = task[1], task[2]
            span = pl.ds(start, size)
            for step in range(1, row_count):
                peer = lax.rem(me_row + step, row_count)
                copy = pltpu.make_async_remote_copy(
                    src_ref=source.at[peer, span],
                    dst_ref=target.at[me_row],
                    send_sem=send_sem.at[step - 1],
                    recv_sem=recv_sem.at[step - 1],
                    device_id=(peer, me_col),
                    device_id_type=MESH,
                )
                copy.start()
                pending.append(copy)
            local.append((source.at[me_row, span], target.at[me_row], bounce, local_sem))

    for here, there, bounce, sem in local:
        copy = pltpu.make_async_copy(here, bounce, sem)
        copy.start()
        copy.wait()
        copy = pltpu.make_async_copy(bounce, there, sem)
        copy.start()
        copy.wait()

    for copy, target, origin, span, slot, pair_send, pair_recv in forwards:
        copy.wait_recv()
        if paired:
            onward = pltpu.make_async_remote_copy(
                src_ref=target.at[origin, span],
                dst_ref=target.at[origin, span],
                send_sem=pair_send.at[1 + slot],
                recv_sem=pair_recv.at[1 + slot],
                device_id=(me_row, partner),
                device_id_type=MESH,
            )
            onward.start()
            pending.append(onward)
    for item in forwards:
        item[0].wait_send()
    for copy in pending:
        copy.wait()


def communicate(tasks, sources, ident):
    row_count, col_count = lax.axis_size("row"), lax.axis_size("col")
    outs, scratch = [], []
    for task, source in zip(tasks, sources):
        if task[0] == "gather":
            shape = (col_count,) + source.shape
            slots = col_count * SUBS
            block = source.shape
        else:
            shape = (row_count, task[2], source.shape[2])
            slots = row_count
            block = shape[1:]
        outs.append(jax.ShapeDtypeStruct(shape, source.dtype))
        scratch += [
            pltpu.VMEM(block, source.dtype),
            pltpu.SemaphoreType.DMA,
            pltpu.SemaphoreType.DMA((slots,)),
            pltpu.SemaphoreType.DMA((slots,)),
            pltpu.SemaphoreType.DMA((slots + 1,)),
            pltpu.SemaphoreType.DMA((slots + 1,)),
        ]
    return pl.pallas_call(
        functools.partial(comm_kernel, tasks, row_count, col_count),
        out_shape=outs,
        in_specs=[pl.BlockSpec(memory_space=pl.ANY)] * len(tasks),
        out_specs=[pl.BlockSpec(memory_space=pl.ANY)] * len(tasks),
        scratch_shapes=scratch,
        compiler_params=pltpu.CompilerParams(
            collective_id=ident, has_side_effects=True, vmem_limit_bytes=VMEM_LIMIT
        ),
        name=f"comm_{ident}",
    )(*sources)


def second_kernel(slots, per, cols_ref, x_ref, tile_ref, inv_ref, out_ref):
    tile = tile_ref.shape[2]
    shard = x_ref.shape[2] // tile

    @pl.loop(0, out_ref.shape[0])
    def _(group):
        for inner in range(per):
            j = group * per + inner
            total = None
            for s in range(slots):
                column = cols_ref[j * slots + s]
                owner = column // shard
                start = pl.multiple_of((column - owner * shard) * tile, tile)
                term = jnp.dot(
                    x_ref[owner, :, pl.ds(start, tile)], tile_ref[j, s], preferred_element_type=jnp.float32
                )
                total = term if total is None else total + term
            out_ref[group, :, inner * tile : (inner + 1) * tile] = (total * inv_ref[j]).astype(jnp.bfloat16)


def second_product(gathered, tiles, columns, inverse, groups):
    col_count, rows, width = gathered.shape
    blocks, slots, tile, _ = tiles.shape
    steps = divisor(rows, 2, 16)
    size = rows // steps
    return pl.pallas_call(
        functools.partial(second_kernel, slots, blocks // groups),
        out_shape=jax.ShapeDtypeStruct((groups, rows, width // groups), jnp.bfloat16),
        grid_spec=pltpu.PrefetchScalarGridSpec(
            num_scalar_prefetch=1,
            grid=(steps,),
            in_specs=[
                pl.BlockSpec((col_count, size, width), lambda i, c: (0, i, 0)),
                pl.BlockSpec(tiles.shape, lambda i, c: (0, 0, 0, 0)),
                pl.BlockSpec(inverse.shape, lambda i, c: (0, 0, 0)),
            ],
            out_specs=pl.BlockSpec((groups, size, width // groups), lambda i, c: (0, i, 0)),
        ),
        compiler_params=pltpu.CompilerParams(vmem_limit_bytes=VMEM_LIMIT),
        name="second_product",
    )(columns, gathered, tiles, inverse)


def first_kernel(slots, parts, cols_ref, tile_ref, *refs):
    pieces, (out_ref, sum_ref, slab, sems) = refs[:parts], refs[parts:]
    step = pl.program_id(0)
    per, tile = tile_ref.shape[0], tile_ref.shape[2]
    in_part = slab.shape[2] // tile

    @pl.when(step == 0)
    def _():
        copies = [pltpu.make_async_copy(piece, slab.at[k], sems.at[k]) for k, piece in enumerate(pieces)]
        for copy in copies:
            copy.start()
        for copy in copies:
            copy.wait()
        sum_ref[...] = jnp.zeros_like(sum_ref)

    for inner in range(per):
        total, weight = None, None
        for s in range(slots):
            column = cols_ref[(step * per + inner) * slots + s]
            owner = column // (in_part * parts)
            rest = column - owner * (in_part * parts)
            part = rest // in_part
            start = pl.multiple_of((rest - part * in_part) * tile, tile)
            block = tile_ref[inner, s]
            term = jnp.dot(block, slab[part, owner, pl.ds(start, tile), :], preferred_element_type=jnp.float32)
            total = term if total is None else total + term
            wide = block.astype(jnp.float32)
            weight = wide if weight is None else weight + wide
        inverse = 1.0 / jnp.sum(weight, axis=1, keepdims=True)
        result = (total * inverse).astype(jnp.bfloat16)
        out_ref[inner * tile : (inner + 1) * tile, :] = result
        sum_ref[...] += jnp.sum(result.astype(jnp.float32).reshape(-1, 8, result.shape[1]), axis=0)


def first_product(pieces, tiles, columns):
    owners, size, width = pieces[0].shape
    blocks, slots, tile, _ = tiles.shape
    per = 4 if blocks % 4 == 0 else 1
    parts = len(pieces)
    return pl.pallas_call(
        functools.partial(first_kernel, slots, parts),
        out_shape=[
            jax.ShapeDtypeStruct((blocks * tile, width), jnp.bfloat16),
            jax.ShapeDtypeStruct((8, width), jnp.float32),
        ],
        grid_spec=pltpu.PrefetchScalarGridSpec(
            num_scalar_prefetch=1,
            grid=(blocks // per,),
            in_specs=[pl.BlockSpec((per, slots, tile, tile), lambda i, c: (i, 0, 0, 0))]
            + [pl.BlockSpec(memory_space=pl.ANY)] * parts,
            out_specs=[
                pl.BlockSpec((per * tile, width), lambda i, c: (i, 0)),
                pl.BlockSpec((8, width), lambda i, c: (0, 0)),
            ],
            scratch_shapes=[
                pltpu.VMEM((parts, owners, size, width), jnp.bfloat16),
                pltpu.SemaphoreType.DMA((parts,)),
            ],
        ),
        compiler_params=pltpu.CompilerParams(vmem_limit_bytes=VMEM_LIMIT),
        name="first_product",
    )(columns, tiles, *pieces)


def mix_kernel(mean_ref, p_ref, prior_ref, out_ref):
    groups, _, width = p_ref.shape
    for group in range(groups):
        part = slice(group * width, (group + 1) * width)
        mixed = mixing * p_ref[group].astype(jnp.float32) + (1.0 - mixing) * prior_ref[:, part]
        out_ref[:, part] = (mixed / mean_ref[0]).astype(out_ref.dtype)


def mix(mean, returned, prior, start, dtype):
    groups, rows, width = returned.shape
    size = rows // divisor(rows, rows // 64, 16) if rows > 64 else rows
    if start % size:
        size = 16
    first = start // size
    return pl.pallas_call(
        mix_kernel,
        out_shape=jax.ShapeDtypeStruct((rows, prior.shape[1]), dtype),
        grid=(rows // size,),
        in_specs=[
            pl.BlockSpec(memory_space=pltpu.SMEM),
            pl.BlockSpec((groups, size, width), lambda i: (0, i, 0)),
            pl.BlockSpec((size, prior.shape[1]), lambda i: (i + first, 0)),
        ],
        out_specs=pl.BlockSpec((size, prior.shape[1]), lambda i: (i, 0)),
        compiler_params=pltpu.CompilerParams(vmem_limit_bytes=VMEM_LIMIT),
        name="mix",
    )(mean, returned, prior)


def local(prior, tiles_first, columns_first, tiles_second, columns_second):
    row_count, col_count = lax.axis_size("row"), lax.axis_size("col")
    rows, width = prior.shape
    tile = tiles_first.shape[2]
    cells = float(rows * row_count * width * col_count)
    slab = width // row_count
    aligned = slab % 128 == 0
    groups = row_count if aligned else 1
    chunks = divisor(rows, CHUNKS, tile)
    size = rows // chunks

    all_first = lax.all_gather(tiles_first, "row", axis=0, tiled=True)
    all_columns = lax.all_gather(columns_first, "row", axis=0, tiled=True).reshape(-1)
    inverse_second = 1.0 / jnp.sum(tiles_second, axis=(1, 3), dtype=jnp.float32)[:, None, :]
    turned = tiles_second.transpose(0, 1, 3, 2)
    columns_second = columns_second.reshape(-1)
    prior_part = jnp.sum(prior)

    def product(gathered):
        mixed = second_product(gathered, turned, columns_second, inverse_second, groups)
        if not aligned:
            mixed = mixed.reshape(size, row_count, slab).transpose(1, 0, 2)
        return mixed

    def widen(returned):
        if not aligned:
            returned = returned.transpose(1, 0, 2).reshape(1, -1, width)
        return returned

    ident = 0
    propagated = mean = prior_sum = None
    for iteration in range(ITERS):
        state, ready, pieces = {}, {}, {}
        if iteration == 0:
            state = {
                k: lax.slice_in_dim(prior, k * size, (k + 1) * size).astype(jnp.bfloat16) for k in range(chunks)
            }
        for time in range(0 if iteration else 1, chunks + 2):
            tasks, sources, where = [], [], []
            if iteration and time < chunks:
                tasks.append(("swap", time * size, size))
                sources.append(propagated)
                where.append(("back", time))
            if 0 <= time - 1 < chunks:
                tasks.append(("gather",))
                sources.append(state[time - 1])
                where.append(("gather", time - 1))
            if 0 <= time - 2 < chunks:
                tasks.append(("swap", 0, size))
                sources.append(ready[time - 2])
                where.append(("on", time - 2))
            results = communicate(tuple(tasks), sources, ident)
            ident += 1
            for (kind, k), result in zip(where, results):
                if kind == "back":
                    state[k] = mix(mean, widen(result), prior, k * size, jnp.bfloat16)
                elif kind == "gather":
                    ready[k] = product(result)
                else:
                    pieces[k] = result
        propagated, part = first_product([pieces[k] for k in range(chunks)], all_first, all_columns)
        propagated = propagated.reshape(row_count, rows, slab)
        part = jnp.sum(part)
        if iteration == 0:
            slab_sum, prior_sum = lax.psum((part, prior_part), ("row", "col"))
        else:
            slab_sum = lax.psum(part, ("row", "col"))
        mean = ((mixing * slab_sum + (1.0 - mixing) * prior_sum) / cells).reshape(1)
    (returned,) = communicate((("swap", 0, rows),), [propagated], ident)
    return mix(mean, widen(returned), prior, 0, jnp.float32)


def solution(mesh):
    return jax.shard_map(
        local,
        mesh=mesh,
        in_specs=(
            P("row", "col"),
            P("row", None, None, None),
            P("row", None),
            P("col", None, None, None),
            P("col", None),
        ),
        out_specs=P("row", "col"),
        check_vma=False,
    )
```

time: 1970 us -> 1360 us (0.69)
  Pallas kernels: 0 us -> 1190 us
  blocking collectives: 939 us -> 111 us
  waiting for transfers between devices: 453 us -> 0.73 us
  local copies, waits for them, and re-layouts: 293 us -> 12.4 us
  matrix products: 113 us -> 0 us
  other arithmetic: 125 us -> 20.4 us
  starting transfers between devices: 21.4 us -> 0.01 us
    pallas_call x0 -> x27, Pallas kernels: none -> 1190 us  [the longest x12 993 us: communicate(): pl.pallas_call(functools.partial(comm_kernel, tasks, row_count, col_count...]
    all_gather x3 -> x1, waiting for transfers between devices: 453 us -> 0.02 us  [local(): all_first = lax.all_gather(tiles_first, 'row', axis=0, tiled=True)]
    psum x2, blocking collectives: 444 us -> 81.8 us  [the longest x1 41.3 us: local(): slab_sum, prior_sum = lax.psum((part, prior_part), ('row', 'col'))]
    all_gather x1, blocking collectives: 287 us -> 29.2 us  [local(): lax.all_gather(columns_first, 'row', axis=0, tiled=True).reshape(-1)]
    all_to_all x1 -> x0, blocking collectives: 207 us -> none  [local(): lax.all_to_all(mixed_cols, 'row', split_axis=0, concat_axis=1, tiled=True)]
    gather x4 -> x0, local copies, waits for them, and re-layouts: 117 us -> none  [the longest x2 69.8 us: second_product(): picked = jnp.take(blocks, columns, axis=0)]
    dot_general x4 -> x0, matrix products: 113 us -> none  [the longest x2 62.6 us: first_product(): jnp.einsum('cisk,isok->cio', picked, tile_set, preferred_element_type=jnp...]
    all_gather x3 -> x1, local copies, waits for them, and re-layouts: 97.6 us -> 0.14 us  [local(): lax.all_gather(columns_first, 'row', axis=0, tiled=True).reshape(-1)]
  transfers between devices with their start and end apart: 6 -> 1, of which waited for: 2 -> 0; matrix products, arithmetic and copies ran while one was open for 8% -> 2% of each run, Pallas kernels for 0% -> 29%
where the time goes in v1:
time: 1360 us; the launch traced here: 1350 us
  Pallas kernels  1190 us (88%)
  blocking collectives  111 us (8%)
  other arithmetic  20.4 us (1%)
  between operations  15.6 us (1%)
    pallas_call x12, Pallas kernels, communicate(): pl.pallas_call(functools.partial(comm_kernel, tasks, row_count, col_count...  993 us
    pallas_call x8, Pallas kernels, second_product(): pl.pallas_call(functools.partial(second_kernel, slots, blocks // groups),...  90.2 us
    pallas_call x2, Pallas kernels, first_product(): pl.pallas_call(functools.partial(first_kernel, slots, parts), out_shape=[...  59.7 us
    pallas_call x5, Pallas kernels, mix(): pl.pallas_call(mix_kernel, out_shape=jax.ShapeDtypeStruct((rows, prior.sh...  49.6 us
    psum x1, blocking collectives, local(): slab_sum, prior_sum = lax.psum((part, prior_part), ('row', 'col'))  41.3 us
    psum x1, blocking collectives, local(): slab_sum = lax.psum(part, ('row', 'col'))  40.5 us
    all_gather x1, blocking collectives, local(): lax.all_gather(columns_first, 'row', axis=0, tiled=True).reshape(-1)  29.2 us
  transfers between devices with their start and end apart: 1, of which 0 were waited for; matrix products, arithmetic and copies ran while one was open for 2% of the time, Pallas kernels for 29%

profile of v1, /device:TPU:10, one launch (start us, length us, event | category | flops | bytes accessed | tf_op | source)
XLA Modules:
  0.0 1352.8 jit_solution(13611256209238051269)
XLA Ops:
  6.5 0.0 all-gather.3.cloned.1.call-start
  6.5 0.7 all-gather.3.cloned.1.call-update
  7.3 0.8 copy.12
  8.0 0.7 reshape.29.cols_ref
  8.7 29.2 %all-gather = s32[8,12,5]{1,2,0:T(8,128)S(1)} all-gather(s32[1,12,5]{1,2,0:T(8,128)} %bitcast.28), channel_id=1, replica_groups=mesh['row'=8,'col'=4] {'row'}, dimensions={0}, use_global_device_ids=true | all-gather | bytes 2160 | tf_op jit(solution)/shard_map/all_gather | solution.py:314
  37.9 0.1 copy.11
  38.0 0.8 reshape.28.cols_ref
  38.8 6.3 copy.13
  45.1 17.2 %fusion = (f32[]{:T(128)}, bf16[1536,3072]{1,0:T(8,128)(2,1)S(1)}) fusion(f32[1536,3072]{1,0:T(8,128)} %prior_ref.9), kind=kLoop, calls=%fused_computation.2 | loop fusion | flops 9437183 | bytes 28311556 | tf_op jit(solution)/shard_map/reduce_sum | solution.py:318
  62.3 3.7 fusion.1
  66.1 0.0 copy-start
  66.1 56.4 %comm_0.1.x_ref = bf16[4,384,3072]{2,1,0:T(8,128)(2,1)} custom-call(bf16[384,3072]{1,0:T(8,128)(2,1)} %get-tuple-element.51.refs_0_), custom_call_target="tpu_custom_call" | custom-call | tf_op jit(solution)/shard_map/comm_0/pallas_call | solution.py:153
  122.5 0.0 copy-done
  122.5 0.6 convert_reduce_fusion
  123.1 0.6 broadcast_divide_fusion
  123.7 11.3 second_product.8.refs_1_
  135.0 122.4 %comm_1.1 = (bf16[4,384,3072]{2,1,0:T(8,128)(2,1)}, bf16[8,384,384]{2,1,0:T(8,128)(2,1)}) custom-call(bf16[384,3072]{1,0:T(8,128)(2,1)} %get-tuple-element.52.refs_0_, bf16[8,384,384]{2,1,0:T(8,128)(2,1)} %second_product.8.refs_1_), custom_call_target="tpu_custom_call" | custom-call | tf_op jit(solution)/shard_map/comm_1/pallas_call | solution.py:153
  257.4 11.3 second_product.9.refs_1_
  268.7 57.6 %comm_2.1 = (bf16[4,384,3072]{2,1,0:T(8,128)(2,1)}, bf16[8,384,384]{2,1,0:T(8,128)(2,1)}) custom-call(bf16[384,3072]{1,0:T(8,128)(2,1)} %get-tuple-element.50.refs_0_, bf16[8,384,384]{2,1,0:T(8,128)(2,1)} %second_product.9.refs_1_), custom_call_target="tpu_custom_call" | custom-call | tf_op jit(solution)/shard_map/comm_2/pallas_call | solution.py:153
  326.4 11.3 second_product.10.refs_1_
  337.6 57.6 %comm_3.1 = (bf16[4,384,3072]{2,1,0:T(8,128)(2,1)}, bf16[8,384,384]{2,1,0:T(8,128)(2,1)}) custom-call(bf16[384,3072]{1,0:T(8,128)(2,1)} %get-tuple-element.49.refs_0_, bf16[8,384,384]{2,1,0:T(8,128)(2,1)} %second_product.10.refs_1_), custom_call_target="tpu_custom_call" | custom-call | tf_op jit(solution)/shard_map/comm_3/pallas_call | solution.py:153
  395.3 11.2 second_product.11.refs_0_
  406.5 56.0 %comm_4.1.refs_3_ = bf16[8,384,384]{2,1,0:T(8,128)(2,1)} custom-call(bf16[8,384,384]{2,1,0:T(8,128)(2,1)} %second_product.11.refs_0_), custom_call_target="tpu_custom_call" | custom-call | tf_op jit(solution)/shard_map/comm_4/pallas_call | solution.py:153
  462.5 0.0 all-gather.3.cloned.1.call-done.tile_ref
  462.5 29.8 %first_product.2 = (bf16[12288,384]{1,0:T(8,128)(2,1)}, f32[8,384]{1,0:T(8,128)}) custom-call(s32[480]{0:T(512)} %reshape.28.cols_ref, bf16[96,5,128,128]{3,2,1,0:T(8,128)(2,1)} %all-gather.3.cloned.1.call-done.tile_ref, bf16[8,384,384]{2,1,0:T(8,128)(2,1)} %get-tuple-element.25.refs_0_, bf16[8,384,384]{2,1,0:T(8,128)(2,1)} %get-tuple-element.27.refs_1_, ...), custom_call_target="tpu_custom_call" | custom-call | tf_op jit(solution)/shard_map/first_product/pallas_call | solution.py:248
  492.4 0.0 copy-start.1
  492.4 55.2 %comm_5.1.p_ref = bf16[8,384,384]{2,1,0:T(8,128)(2,1)} custom-call(bf16[8,1536,384]{2,1,0:T(8,128)(2,1)} %bitcast.15), custom_call_target="tpu_custom_call" | custom-call | tf_op jit(solution)/shard_map/comm_5/pallas_call | solution.py:153
  547.5 0.0 copy-done.1
  547.6 0.6 reduce_sum.37
  548.2 41.3 %all-reduce = (f32[]{:T(128)}, f32[]{:T(128)}) all-reduce(f32[]{:T(128)} %reduce_sum.37, f32[]{:T(128)} %get-tuple-element.47), channel_id=1, replica_groups=mesh['row'=8,'col'=4] {'row','col'}, use_global_device_ids=true, to_apply=%region_2.0 | all-reduce | flops 2 | bytes 16 | tf_op jit(solution)/shard_map/psum | solution.py:366
  590.8 6.2 mix.5.refs_1_
  597.0 56.8 %comm_6.1 = (bf16[8,384,384]{2,1,0:T(8,128)(2,1)}, bf16[4,384,3072]{2,1,0:T(8,128)(2,1)}) custom-call(bf16[8,1536,384]{2,1,0:T(8,128)(2,1)} %bitcast.16, bf16[384,3072]{1,0:T(8,128)(2,1)} %mix.5.refs_1_), custom_call_target="tpu_custom_call" | custom-call | tf_op jit(solution)/shard_map/comm_6/pallas_call | solution.py:153
  653.8 6.2 mix.6.refs_1_
  659.9 11.3 second_product.12.refs_2_
  671.2 106.9 %comm_7.1 = (bf16[8,384,384]{2,1,0:T(8,128)(2,1)}, bf16[4,384,3072]{2,1,0:T(8,128)(2,1)}, bf16[8,384,384]{2,1,0:T(8,128)(2,1)}) custom-call(bf16[8,1536,384]{2,1,0:T(8,128)(2,1)} %bitcast.17, bf16[384,3072]{1,0:T(8,128)(2,1)} %mix.6.refs_1_, bf16[8,384,384]{2,1,0:T(8,128)(2,1)} %second_product.12.refs_2_), custom_call_target="tpu_custom_call" | custom-call | tf_op jit(solution)/shard_map/comm_7/pallas_call | solution.py:153
  778.1 6.2 mix.7.refs_1_
  784.3 11.3 second_product.13.refs_2_
  795.6 106.3 %comm_8.1 = (bf16[8,384,384]{2,1,0:T(8,128)(2,1)}, bf16[4,384,3072]{2,1,0:T(8,128)(2,1)}, bf16[8,384,384]{2,1,0:T(8,128)(2,1)}) custom-call(bf16[8,1536,384]{2,1,0:T(8,128)(2,1)} %bitcast.18, bf16[384,3072]{1,0:T(8,128)(2,1)} %mix.7.refs_1_, bf16[8,384,384]{2,1,0:T(8,128)(2,1)} %second_product.13.refs_2_), custom_call_target="tpu_custom_call" | custom-call | tf_op jit(solution)/shard_map/comm_8/pallas_call | solution.py:153
  901.9 6.2 mix.8.refs_0_
  908.1 11.3 second_product.14.refs_1_
  919.4 56.8 %comm_9.1 = (bf16[4,384,3072]{2,1,0:T(8,128)(2,1)}, bf16[8,384,384]{2,1,0:T(8,128)(2,1)}) custom-call(bf16[384,3072]{1,0:T(8,128)(2,1)} %mix.8.refs_0_, bf16[8,384,384]{2,1,0:T(8,128)(2,1)} %second_product.14.refs_1_), custom_call_target="tpu_custom_call" | custom-call | tf_op jit(solution)/shard_map/comm_9/pallas_call | solution.py:153
  976.1 11.2 second_product.15.refs_0_
  987.4 55.9 %comm_10.1.refs_3_ = bf16[8,384,384]{2,1,0:T(8,128)(2,1)} custom-call(bf16[8,384,384]{2,1,0:T(8,128)(2,1)} %second_product.15.refs_0_), custom_call_target="tpu_custom_call" | custom-call | tf_op jit(solution)/shard_map/comm_10/pallas_call | solution.py:153
  1043.3 29.8 %first_product.3 = (bf16[12288,384]{1,0:T(8,128)(2,1)}, f32[8,384]{1,0:T(8,128)}) custom-call(s32[480]{0:T(512)} %reshape.28.cols_ref, bf16[96,5,128,128]{3,2,1,0:T(8,128)(2,1)} %all-gather.3.cloned.1.call-done.tile_ref, bf16[8,384,384]{2,1,0:T(8,128)(2,1)} %get-tuple-element.35.refs_0_, bf16[8,384,384]{2,1,0:T(8,128)(2,1)} %get-tuple-element.38.refs_1_, ...), custom_call_target="tpu_custom_call" | custom-call | tf_op jit(solution)/shard_map/first_product/pallas_call | solution.py:248
  1073.1 1.4 reduce_sum.39
  1074.5 40.5 %psum.23 = f32[]{:T(128)} all-reduce(f32[]{:T(128)} %reduce_sum.39), channel_id=1, replica_groups=mesh['row'=8,'col'=4] {'row','col'}, use_global_device_ids=true, to_apply=%region_6.0 | all-reduce | flops 1 | bytes 8 | tf_op jit(solution)/shard_map/psum | solution.py:368
  1115.7 205.5 %comm_11.1.p_ref = bf16[8,1536,384]{2,1,0:T(8,128)(2,1)} custom-call(bf16[8,1536,384]{2,1,0:T(8,128)(2,1)} %bitcast.19), custom_call_target="tpu_custom_call" | custom-call | tf_op jit(solution)/shard_map/comm_11/pallas_call | solution.py:153
  1321.2 24.8 %mix.9 = f32[1536,3072]{1,0:T(8,128)} custom-call(f32[1]{0:T(128)} %bitcast.5.mean_ref, bf16[8,1536,384]{2,1,0:T(8,128)(2,1)} %comm_11.1.p_ref, f32[1536,3072]{1,0:T(8,128)} %prior_ref.9), custom_call_target="tpu_custom_call" | custom-call | tf_op jit(solution)/shard_map/mix/pallas_call | solution.py:287
Async XLA Ops:
  6.5 456.0 %all-gather.3.cloned.1.call-start = ((), (), s32[]{:S(2)}) async-start(), calls=%async_computation | async-start | bytes 17694720 | tf_op jit(solution)/shard_map/all_gather | solution.py:313
  66.1 56.4 %copy-start = (bf16[24,5,128,128]{3,2,1,0:T(8,128)(2,1)S(1)}, bf16[24,5,128,128]{3,2,1,0:T(8,128)(2,1)}, u32[]{:S(2)}) copy-start(bf16[24,5,128,128]{3,2,1,0:T(8,128)(2,1)} %param.8) | copy-start | bytes 11796484
  492.4 55.2 %copy-start.1 = (f32[8,384]{1,0:T(8,128)S(1)}, f32[8,384]{1,0:T(8,128)}, u32[]{:S(2)}) copy-start(f32[8,384]{1,0:T(8,128)} %get-tuple-element.32) | copy-start | bytes 36868
Sparse Core Ops, SparseCore 0:
  9.5 260.8 all-gather.2
